TPU v7x, 256 devices: a whole 4x4x8 slice. The times are simulated.
256 devices in a mesh: area: 32 (over y, x, core), rank: 8 (over z).
Axes of the slice: x: 4, y: 4, z: 8, core: 2. Of those that a mesh axis runs over, the one named last changes fastest.
Arguments:
- initial_bits: int32 [2, 48, 1024], P(None, None, ('area', 'rank')), may hold values from -2147483648 to 2147483646
- membrane: float32 [48, 32768], P(None, ('area', 'rank')), may hold values from -100 to 200
- drive: int32 [32768], P(('area', 'rank')), may hold values from 0 to 47
- leak_shift: int32 [32768], P(('area', 'rank')), may hold values from 2 to 5
- weights: bfloat16 [256, 128, 128, 128], P(('area', 'rank')), may hold values from -3 to 3, as said below
- pre_block: int32 [256, 128], P(('area', 'rank')), may hold values from 0 to 255
- block_mask: int32 [256, 128], P(('area', 'rank')), may hold values 0 or 1
- delay: int32 [256, 128], P(('area', 'rank')), may hold values from 2 to 5
- area_of_block: int32 [256, 1], replicated, may hold values from 0 to 31
Outputs:
- final_membrane: float32 [48, 32768], P(None, ('area', 'rank'))
- area_rates: float32 [10, 32], replicated
Inputs may be any that keep to these rules, and one draw needn't show every extreme that they name: weights hold whole numbers. `area_of_block`: every area holds at least one block.
All inputs are finite; a program needn't handle non-finite values. No bound on the sum of `block_mask` on one device may be relied on, other than what follows from the above.
Results may differ from a plain program's by a relative error of at most 0.0003.
Values sent between devices are 32-bit elements; how exact they have to be, the bound alone decides.
A program may use at most 128 MiB of HBM per device.

v0:
```python
import jax
import jax.numpy as jnp
from jax import lax
from jax.sharding import Mesh
from jax.sharding import PartitionSpec as P

AREAS = 32
DMIN = 2
NDELAY = 4
STEPS = 10
AREA = ("area_0", "area_1", "area_2")
AREA_RANK = ("area_0", "area_1", "area_2", "rank")


threshold_level = 200.0


def laid_out(pieces, dim):
    pieces = jnp.moveaxis(pieces, 0, dim)
    dims = pieces.shape
    return pieces.reshape(*dims[:dim], dims[dim] * dims[dim + 1], *dims[dim + 2 :])


def from_everyone(shard, axis):
    copies = jnp.broadcast_to(shard, (lax.axis_size(axis), *shard.shape))
    return lax.all_to_all(copies, axis, split_axis=0, concat_axis=0, tiled=True)


def gathered_copies(shard, axis, dim):
    return laid_out(from_everyone(shard, axis), dim)


def by_axis(shard, axes):
    for axis in axes:
        shard = lax.psum(shard, axis)
    return shard


def unpack(packed):
    shifts = jnp.arange(32, dtype=jnp.int32)
    bit_values = jnp.bitwise_and(jnp.right_shift(packed[..., None], shifts), 1)
    return bit_values.reshape(packed.shape[:-1] + (packed.shape[-1] * 32,))


def pack_bits(current_spike_flags):
    trials, width = current_spike_flags.shape
    bit_values = current_spike_flags.astype(jnp.int32).reshape(trials, width // 32, 32)
    rolled_history = jnp.left_shift(bit_values, jnp.arange(32, dtype=jnp.int32))
    return jnp.sum(rolled_history, axis=-1, dtype=jnp.int32)


def collect(packed):
    within = gathered_copies(packed, "rank", 2)
    return gathered_copies(within, AREA, 2)


def on_device(
    initial_bits, membrane, drive, leak_shift, weights, pre_block, block_mask, delay, area_of_block
):
    blk_dev, slots, block = (weights.shape[0], weights.shape[1], weights.shape[2])
    trials, width = membrane.shape
    intervals = STEPS // DMIN
    rows_all = DMIN * trials
    lag_table = (
        delay[:, :, None] - DMIN == jnp.arange(NDELAY, dtype=jnp.int32)[None, None, :]
    ).astype(jnp.float32)
    input_weighting = block_mask.astype(jnp.float32)[:, :, None] * lag_table
    lag_mask = jnp.transpose(input_weighting.astype(jnp.bfloat16), (0, 2, 1))[:, :, None, :, None]
    flat_weights = weights.reshape(blk_dev, slots * block, block)
    buffer = jnp.zeros((STEPS + NDELAY, trials, width), jnp.float32)
    history = initial_bits
    membrane_voltage = jnp.floor(membrane)
    leak_scale = 1.0 / jnp.left_shift(jnp.ones_like(leak_shift), leak_shift).astype(jnp.float32)
    drive_float = drive.astype(jnp.float32)
    fired_steps = []
    kept = []
    for interval in range(intervals):
        gathered = collect(history)
        kept.append(gathered)
        total_blocks = gathered.shape[2] * 32 // block
        source_rows = gathered.reshape(rows_all, total_blocks, block // 32)
        picked = jnp.take(source_rows, pre_block.reshape(blk_dev * slots), axis=1)
        selected = unpack(picked).astype(jnp.bfloat16).reshape(rows_all, blk_dev, slots, block)
        selected = jnp.transpose(selected, (1, 0, 2, 3))[:, None, :, :, :]
        lagged_rows = (selected * lag_mask).reshape(blk_dev, NDELAY * rows_all, slots * block)
        product = jnp.einsum(
            "brx,bxy->bry", lagged_rows, flat_weights, preferred_element_type=jnp.float32
        )
        arrived = product.reshape(blk_dev, NDELAY, DMIN, trials, block)
        arrived = jnp.transpose(arrived, (1, 2, 3, 0, 4)).reshape(NDELAY, DMIN, trials, width)
        first_step = (interval - 1) * DMIN
        for lag_index in range(NDELAY):
            for offset in range(DMIN):
                landing = first_step + offset + DMIN + lag_index
                buffer = buffer.at[landing].add(arrived[lag_index, offset])
        packed_list = []
        for offset in range(DMIN):
            current = buffer[interval * DMIN + offset]
            membrane_voltage = (
                membrane_voltage - jnp.floor(membrane_voltage * leak_scale) + current + drive_float
            )
            current_spike_flags = membrane_voltage >= threshold_level
            membrane_voltage = jnp.where(
                current_spike_flags,
                jnp.zeros_like(membrane_voltage),
                jnp.maximum(membrane_voltage, -threshold_level),
            )
            fired_steps.append(current_spike_flags)
            packed_list.append(pack_bits(current_spike_flags))
        history = jnp.stack(packed_list)
    area_table = (area_of_block == jnp.arange(AREAS, dtype=jnp.int32)[None, :]).astype(jnp.float32)
    sizes_per_area = jnp.sum(area_table, axis=0) * (trials * block)
    own_start = lax.axis_index(AREA_RANK) * blk_dev
    own_table = lax.dynamic_slice_in_dim(area_table, own_start, blk_dev, 0)
    block_totals = jnp.stack(
        [
            jnp.sum(
                current_spike_flags.astype(jnp.float32).reshape(trials, blk_dev, block), axis=(0, 2)
            )
            for current_spike_flags in fired_steps
        ]
    )
    partial_counts = jnp.dot(block_totals, own_table, precision=lax.Precision.HIGHEST)
    counts = by_axis(partial_counts, AREA_RANK)
    return (membrane_voltage, counts / sizes_per_area)


def solution(mesh):
    split = Mesh(
        mesh.devices.reshape(4, 4, 2, mesh.shape["rank"]), ("area_0", "area_1", "area_2", "rank")
    )
    return jax.shard_map(
        on_device,
        mesh=split,
        in_specs=(
            P(None, None, AREA_RANK),
            P(None, AREA_RANK),
            P(AREA_RANK),
            P(AREA_RANK),
            P(AREA_RANK, None, None, None),
            P(AREA_RANK, None),
            P(AREA_RANK, None),
            P(AREA_RANK, None),
            P(),
        ),
        out_specs=(P(None, AREA_RANK), P()),
        check_vma=False,
    )
```

profile of v0, /device:TPU:32, one launch (start us, length us, event | category | flops | bytes accessed | tf_op | source)
XLA Modules:
  0.0 469.6 jit_solution(6175274694056865357)
XLA Ops:
  2.0 8.6 %all-to-all-start = ((s32[8,1,384]{2,1,0:T(1,128)}), s32[8,1,384]{2,1,0:T(1,128)S(1)}, u32[]{:S(2)}, u32[]{:S(2)}) async-start(s32[8,1,384]{2,1,0:T(1,128)} %reshape.1665), calls=%async_computation | async-start | bytes 24576 | tf_op jit(solution)/shard_map/all_to_all | solution.py:26
  14.3 2.7 all-to-all-done
  18.8 2.6 reshape.1667
  21.3 7.5 %all-to-all-start.1 = ((s32[32,1,3072]{2,1,0:T(1,128)}), s32[32,1,3072]{2,1,0:T(1,128)S(1)}, u32[]{:S(2)}, u32[]{:S(2)}) async-start(s32[32,1,3072]{2,1,0:T(1,128)} %reshape.1667), calls=%async_computation.1 | async-start | bytes 786432 | tf_op jit(solution)/shard_map/all_to_all | solution.py:26
  28.9 10.2 %all-to-all-done.1 = s32[32,1,3072]{2,1,0:T(1,128)S(1)} async-done(((s32[32,1,3072]{2,1,0:T(1,128)}), s32[32,1,3072]{2,1,0:T(1,128)S(1)}, u32[]{:S(2)}, u32[]{:S(2)}) %all-to-all-start.1) | async-done | bytes 393248 | tf_op jit(solution)/shard_map/all_to_all | solution.py:26
  44.1 3.8 shift_right_arithmetic.145
  47.9 16.9 %shift_right_arithmetic.146 = s32[2,48,16384]{1,0,2:T(2,128)} reshape(s32[96,128,4,32]{0,3,2,1:T(8,128)} %shift_right_arithmetic.145) | data formatting | bytes 12582912 | tf_op jit(solution)/shard_map/shift_right_arithmetic | solution.py:41
  64.8 20.0 %copy.55 = s32[2,48,16384]{2,1,0:T(8,128)} copy(s32[2,48,16384]{1,0,2:T(2,128)} %shift_right_arithmetic.146) | data formatting | bytes 12582912 | tf_op jit(solution)/shard_map/shift_right_arithmetic | solution.py:41
  84.8 3.7 and_convert_fusion.4
  88.8 3.4 fusion.8
  93.4 10.7 %all_to_all.50 = s32[8,1,384]{2,1,0:T(1,128)S(1)} all-to-all(s32[8,1,384]{2,1,0:T(1,128)S(1)} %reshape.1669), channel_id=1, replica_groups=mesh['area_0'=4,'area_1'=4,'area_2'=2,'rank'=8] {'rank'}, dimensions={0} | all-to-all | bytes 24576 | tf_op jit(solution)/shard_map/all_to_all | solution.py:26
  107.3 14.0 %all_to_all.51 = s32[32,1,3072]{2,1,0:T(1,128)S(1)} all-to-all(s32[32,1,3072]{2,1,0:T(1,128)S(1)} %reshape.1671), channel_id=1, replica_groups=mesh['area_0'=4,'area_1'=4,'area_2'=2,'rank'=8] {'area_0','area_1','area..., dimensions={0} | all-to-all | bytes 786432 | tf_op jit(solution)/shard_map/all_to_all | solution.py:26
  126.4 3.8 shift_right_arithmetic.153
  130.2 16.9 %shift_right_arithmetic.154 = s32[2,48,16384]{1,0,2:T(2,128)} reshape(s32[96,128,4,32]{0,3,2,1:T(8,128)} %shift_right_arithmetic.153) | data formatting | bytes 12582912 | tf_op jit(solution)/shard_map/shift_right_arithmetic | solution.py:41
  147.1 20.0 %copy.60 = s32[2,48,16384]{2,1,0:T(8,128)} copy(s32[2,48,16384]{1,0,2:T(2,128)} %shift_right_arithmetic.154) | data formatting | bytes 12582912 | tf_op jit(solution)/shard_map/shift_right_arithmetic | solution.py:41
  167.1 3.7 and_convert_fusion.3
  171.1 3.4 fusion.6
  175.6 10.1 %all_to_all.52 = s32[8,1,384]{2,1,0:T(1,128)S(1)} all-to-all(s32[8,1,384]{2,1,0:T(1,128)S(1)} %reshape.1673), channel_id=1, replica_groups=mesh['area_0'=4,'area_1'=4,'area_2'=2,'rank'=8] {'rank'}, dimensions={0} | all-to-all | bytes 24576 | tf_op jit(solution)/shard_map/all_to_all | solution.py:26
  188.9 13.8 %all_to_all.53 = s32[32,1,3072]{2,1,0:T(1,128)S(1)} all-to-all(s32[32,1,3072]{2,1,0:T(1,128)S(1)} %reshape.1675), channel_id=1, replica_groups=mesh['area_0'=4,'area_1'=4,'area_2'=2,'rank'=8] {'area_0','area_1','area..., dimensions={0} | all-to-all | bytes 786432 | tf_op jit(solution)/shard_map/all_to_all | solution.py:26
  207.8 3.8 shift_right_arithmetic.156
  211.6 16.9 %shift_right_arithmetic.157 = s32[2,48,16384]{1,0,2:T(2,128)} reshape(s32[96,128,4,32]{0,3,2,1:T(8,128)} %shift_right_arithmetic.156) | data formatting | bytes 12582912 | tf_op jit(solution)/shard_map/shift_right_arithmetic | solution.py:41
  228.5 20.0 %copy.65 = s32[2,48,16384]{2,1,0:T(8,128)} copy(s32[2,48,16384]{1,0,2:T(2,128)} %shift_right_arithmetic.157) | data formatting | bytes 12582912 | tf_op jit(solution)/shard_map/shift_right_arithmetic | solution.py:41
  248.5 3.7 and_convert_fusion.2
  252.5 3.4 fusion.4
  257.7 4.7 all-to-all-start.6
  262.4 6.2 %all-to-all-done.6 = s32[8,1,384]{2,1,0:T(1,128)S(1)} async-done(((s32[8,1,384]{2,1,0:T(1,128)}), s32[8,1,384]{2,1,0:T(1,128)S(1)}, u32[]{:S(2)}, u32[]{:S(2)}) %all-to-all-start.6) | async-done | bytes 12320 | tf_op jit(solution)/shard_map/all_to_all | solution.py:26
  270.0 2.6 reshape.1679
  272.6 4.1 all-to-all-start.7
  276.8 10.1 %all-to-all-done.7 = s32[32,1,3072]{2,1,0:T(1,128)S(1)} async-done(((s32[32,1,3072]{2,1,0:T(1,128)}), s32[32,1,3072]{2,1,0:T(1,128)S(1)}, u32[]{:S(2)}, u32[]{:S(2)}) %all-to-all-start.7) | async-done | bytes 393248 | tf_op jit(solution)/shard_map/all_to_all | solution.py:26
  291.9 3.8 shift_right_arithmetic.159
  295.7 16.9 %shift_right_arithmetic.160 = s32[2,48,16384]{1,0,2:T(2,128)} reshape(s32[96,128,4,32]{0,3,2,1:T(8,128)} %shift_right_arithmetic.159) | data formatting | bytes 12582912 | tf_op jit(solution)/shard_map/shift_right_arithmetic | solution.py:41
  312.6 20.0 %copy.70 = s32[2,48,16384]{2,1,0:T(8,128)} copy(s32[2,48,16384]{1,0,2:T(2,128)} %shift_right_arithmetic.160) | data formatting | bytes 12582912 | tf_op jit(solution)/shard_map/shift_right_arithmetic | solution.py:41
  332.6 3.7 and_convert_fusion.1
  336.6 3.4 fusion.2
  341.8 4.7 %all-to-all-start.8 = ((s32[8,1,384]{2,1,0:T(1,128)}), s32[8,1,384]{2,1,0:T(1,128)S(1)}, u32[]{:S(2)}, u32[]{:S(2)}) async-start(s32[8,1,384]{2,1,0:T(1,128)} %reshape.1681), calls=%async_computation.8 | async-start | bytes 24576 | tf_op jit(solution)/shard_map/all_to_all | solution.py:26
  346.5 6.3 %all-to-all-done.8 = s32[8,1,384]{2,1,0:T(1,128)S(1)} async-done(((s32[8,1,384]{2,1,0:T(1,128)}), s32[8,1,384]{2,1,0:T(1,128)S(1)}, u32[]{:S(2)}, u32[]{:S(2)}) %all-to-all-start.8) | async-done | bytes 12320 | tf_op jit(solution)/shard_map/all_to_all | solution.py:26
  354.1 2.6 reshape.1683
  356.7 4.1 all-to-all-start.9
  363.4 7.7 %all-to-all-done.9 = s32[32,1,3072]{2,1,0:T(1,128)S(1)} async-done(((s32[32,1,3072]{2,1,0:T(1,128)}), s32[32,1,3072]{2,1,0:T(1,128)S(1)}, u32[]{:S(2)}, u32[]{:S(2)}) %all-to-all-start.9) | async-done | bytes 393248 | tf_op jit(solution)/shard_map/all_to_all | solution.py:26
  376.1 3.8 shift_right_arithmetic.162
  379.9 16.9 %shift_right_arithmetic.163 = s32[2,48,16384]{1,0,2:T(2,128)} reshape(s32[96,128,4,32]{0,3,2,1:T(8,128)} %shift_right_arithmetic.162) | data formatting | bytes 12582912 | tf_op jit(solution)/shard_map/shift_right_arithmetic | solution.py:41
  396.8 20.0 %copy.75 = s32[2,48,16384]{2,1,0:T(8,128)} copy(s32[2,48,16384]{1,0,2:T(2,128)} %shift_right_arithmetic.163) | data formatting | bytes 12582912 | tf_op jit(solution)/shard_map/shift_right_arithmetic | solution.py:41
  416.8 3.7 and_convert_fusion
  420.8 3.4 fusion
  426.1 6.3 %stack.91 = f32[10,1]{0,1:T(1,128)S(1)} concatenate(f32[1,1]{0,1:T(1,128)} %bitcast.91, f32[1,1]{0,1:T(1,128)} %bitcast.92, f32[1,1]{0,1:T(1,128)} %bitcast.93, f32[1,1]{0,1:T(1,128)} %bitcast.94, f32[1,1]{0,1:T(1,128)} %bitcast.95, f32[1,1]{0,1:T(1,128)} %bitcast.96, f32[1,1]{0,1:T(1,128)} %bitcast.97, f32[1,1]{0,1:T(1,128)} %bitcast.98, f32[1,1]{0,1:T(1,128)} %bitcast.99, ...), dimensions={0} | concatenate | bytes 80 | tf_op jit(solution)/shard_map/stack | solution.py:115
  432.5 8.6 %psum.28 = f32[10,32]{1,0:T(8,128)S(1)} all-reduce(f32[10,32]{1,0:T(8,128)S(1)} %broadcast_multiply_fusion), channel_id=1, replica_groups=mesh['area_0'=4,'area_1'=4,'area_2'=2,'rank'=8] {'area_0'}, use_global_device_ids=true, to_apply=%region_18.20 | all-reduce | flops 320 | bytes 2560 | tf_op jit(solution)/shard_map/psum | solution.py:35
  441.1 9.0 %psum.29 = f32[10,32]{1,0:T(8,128)S(1)} all-reduce(f32[10,32]{1,0:T(8,128)S(1)} %psum.28), channel_id=1, replica_groups=mesh['area_0'=4,'area_1'=4,'area_2'=2,'rank'=8] {'area_1'}, use_global_device_ids=true, to_apply=%region_19.21 | all-reduce | flops 320 | bytes 2560 | tf_op jit(solution)/shard_map/psum | solution.py:35
  452.7 15.8 %psum.31 = f32[10,32]{1,0:T(8,128)S(1)} all-reduce(f32[10,32]{1,0:T(8,128)S(1)} %psum.30), channel_id=1, replica_groups=mesh['area_0'=4,'area_1'=4,'area_2'=2,'rank'=8] {'rank'}, use_global_device_ids=true, to_apply=%region_21.23 | all-reduce | flops 320 | bytes 2560 | tf_op jit(solution)/shard_map/psum | solution.py:35
  (192 shorter events, 55.4 us)
Async XLA Ops:
  0.6 0.7 copy-start
  2.0 14.9 %all-to-all-start = ((s32[8,1,384]{2,1,0:T(1,128)}), s32[8,1,384]{2,1,0:T(1,128)S(1)}, u32[]{:S(2)}, u32[]{:S(2)}) async-start(s32[8,1,384]{2,1,0:T(1,128)} %reshape.1665), calls=%async_computation | async-start | bytes 24576 | tf_op jit(solution)/shard_map/all_to_all | solution.py:26
  21.3 17.7 %all-to-all-start.1 = ((s32[32,1,3072]{2,1,0:T(1,128)}), s32[32,1,3072]{2,1,0:T(1,128)S(1)}, u32[]{:S(2)}, u32[]{:S(2)}) async-start(s32[32,1,3072]{2,1,0:T(1,128)} %reshape.1667), calls=%async_computation.1 | async-start | bytes 786432 | tf_op jit(solution)/shard_map/all_to_all | solution.py:26
  84.8 4.0 copy-start.4
  88.8 3.6 copy-start.2
  167.1 4.0 copy-start.5
  248.5 4.0 copy-start.6
  252.5 9.9 %copy-start.3 = (s32[256,1]{0,1:T(1,128)S(1)}, s32[256,1]{0,1:T(1,128)}, u32[]{:S(2)}) copy-start(s32[256,1]{0,1:T(1,128)} %param.99) | copy-start | bytes 3076
  257.7 11.0 %all-to-all-start.6 = ((s32[8,1,384]{2,1,0:T(1,128)}), s32[8,1,384]{2,1,0:T(1,128)S(1)}, u32[]{:S(2)}, u32[]{:S(2)}) async-start(s32[8,1,384]{2,1,0:T(1,128)} %reshape.1677), calls=%async_computation.6 | async-start | bytes 24576 | tf_op jit(solution)/shard_map/all_to_all | solution.py:26
  272.6 14.3 %all-to-all-start.7 = ((s32[32,1,3072]{2,1,0:T(1,128)}), s32[32,1,3072]{2,1,0:T(1,128)S(1)}, u32[]{:S(2)}, u32[]{:S(2)}) async-start(s32[32,1,3072]{2,1,0:T(1,128)} %reshape.1679), calls=%async_computation.7 | async-start | bytes 786432 | tf_op jit(solution)/shard_map/all_to_all | solution.py:26
  332.6 4.0 copy-start.7
  341.8 11.1 %all-to-all-start.8 = ((s32[8,1,384]{2,1,0:T(1,128)}), s32[8,1,384]{2,1,0:T(1,128)S(1)}, u32[]{:S(2)}, u32[]{:S(2)}) async-start(s32[8,1,384]{2,1,0:T(1,128)} %reshape.1681), calls=%async_computation.8 | async-start | bytes 24576 | tf_op jit(solution)/shard_map/all_to_all | solution.py:26
  356.7 14.3 %all-to-all-start.9 = ((s32[32,1,3072]{2,1,0:T(1,128)}), s32[32,1,3072]{2,1,0:T(1,128)S(1)}, u32[]{:S(2)}, u32[]{:S(2)}) async-start(s32[32,1,3072]{2,1,0:T(1,128)} %reshape.1683), calls=%async_computation.9 | async-start | bytes 786432 | tf_op jit(solution)/shard_map/all_to_all | solution.py:26
  416.8 4.0 copy-start.8
  420.8 48.3 %copy-start.1 = (s32[2,48,4]{1,2,0:T(4,128)S(1)}, s32[2,48,4]{1,2,0:T(4,128)}, u32[]{:S(2)}) copy-start(s32[2,48,4]{1,2,0:T(4,128)} %param.91) | copy-start | bytes 4612
where the time goes:
time: 478 us; the launch traced here: 470 us
  local copies, waits for them, and re-layouts  246 us (51%)
  blocking collectives  84.7 us (18%)
  waiting for transfers between devices  43.1 us (9%)
  other arithmetic  42.7 us (9%)
  starting transfers between devices  33.7 us (7%)
  matrix products  17 us (4%)
    shift_right_arithmetic x18, local copies, waits for them, and re-layouts, unpack(): bit_values = jnp.bitwise_and(jnp.right_shift(packed[..., None], shifts), 1)  203 us
    all_to_all x4, blocking collectives, from_everyone(): return lax.all_to_all(copies, axis, split_axis=0, concat_axis=0, tiled=True)  48.6 us
    all_to_all x6, waiting for transfers between devices, from_everyone(): return lax.all_to_all(copies, axis, split_axis=0, concat_axis=0, tiled=True)  43.1 us
    psum x4, blocking collectives, by_axis(): shard = lax.psum(shard, axis)  36 us
    all_to_all x6, starting transfers between devices, from_everyone(): return lax.all_to_all(copies, axis, split_axis=0, concat_axis=0, tiled=True)  33.7 us
    unnamed x50, local copies, waits for them, and re-layouts  26.9 us
    convert_element_type x5, other arithmetic, on_device(): unpack(picked).astype(jnp.bfloat16).reshape(rows_all, blk_dev, slots, block)  18.7 us
    dot_general x5, matrix products, on_device(): jnp.einsum('brx,bxy->bry', lagged_rows, flat_weights, preferred_element_t...  17 us
  transfers between devices with their start and end apart: 6, of which 6 were waited for; matrix products, arithmetic and copies ran while one was open for 1% of the time, Pallas kernels for 0%

commit v1 on v0

v1 whole, which is shorter than its diff:
```python
import functools

import jax
import jax.numpy as jnp
from jax import lax
from jax.experimental import pallas as pl
from jax.experimental.pallas import tpu as pltpu
from jax.sharding import PartitionSpec as P

AREAS = 32
DMIN = 2
STEPS = 10
THRESHOLD = 200.0
MESH = pl.DeviceIdType.MESH
WORDS = 3
SLOTS_PER_DOT = 4
NX, NY, NC = 4, 4, 2


def batches(nz):
    pairs = [(2 * near - 1, 2) for near in range(1, nz // 2 - 1)]
    return [(0, 1)] + pairs + [(nz - 3, 3)]


def z_place(offset, nz):
    return 2 * (nz - offset) if offset > nz // 2 else max(2 * offset - 1, 0)


def block_place(area, offset, areas, nz):
    place = jnp.where(offset > nz // 2, 2 * (nz - offset), jnp.maximum(2 * offset - 1, 0))
    first = jnp.where(place % 2 == 1, place, place - 1)
    count = jnp.where(place == 0, 1, 2)
    first = jnp.where(place == 0, 0, first)
    last = place >= nz - 3
    first = jnp.where(last, nz - 3, first)
    count = jnp.where(last, 3, count)
    return first * areas + area * count + place - first


def static_row(area, place, areas, nz):
    first, count = next(b for b in batches(nz) if b[0] <= place < b[0] + b[1])
    return (first * areas + area * count + place - first) * WORDS


def ring_hops(step, n):
    return min(step, n - step)


def plane_offsets(ny, nx, nc):
    found = [
        (dy, dx, dc)
        for dy in range(ny)
        for dx in range(nx)
        for dc in range(nc)
        if (dy, dx, dc) != (0, 0, 0)
    ]
    return sorted(found, key=lambda o: -(ring_hops(o[0], ny) + ring_hops(o[1], nx)))


def kernel(
    dims,
    pre_ref,
    mask_ref,
    delay_ref,
    bits_ref,
    membrane_ref,
    drive_ref,
    leak_ref,
    area_ref,
    weights_hbm,
    out_membrane,
    out_rates,
    weights,
    landing,
    words,
    volt,
    counts,
    tile,
    columns,
    totals,
    base0,
    base1,
    stride,
    odd,
    weights_sem,
    send_sem,
    z_sem,
    plane_sem,
    last_send_sem,
    last_z_sem,
    last_plane_sem,
):
    ny, nx, nc, nz, slots, trials, steps = dims
    areas = ny * nx * nc
    blocks = areas * nz
    per_interval = blocks * WORDS
    intervals = steps // DMIN
    area = lax.axis_index("area")
    rank = lax.axis_index("rank")
    y, x, core = area // (nx * nc), (area // nc) % nx, area % nc
    offsets = plane_offsets(ny, nx, nc)

    def plane_peer(offset):
        dy, dx, dc = offset
        there = (((y + dy) % ny) * nx + (x + dx) % nx) * nc + (core + dc) % nc
        return (there, rank)

    def z_peer(dz):
        return (area, (rank + dz) % nz)

    peers = [z_peer(dz) for dz in range(1, nz)] + [plane_peer(o) for o in offsets]
    barrier = pltpu.get_barrier_semaphore()
    for peer in peers:
        pl.semaphore_signal(barrier, inc=1, device_id=peer, device_id_type=MESH)

    load_weights = pltpu.make_async_copy(weights_hbm, weights, weights_sem)
    load_weights.start()

    def index_slot(k, carry):
        d, keep, pre = delay_ref[k], mask_ref[k], pre_ref[k]
        place = block_place(pre // nz, (pre % nz - rank + nz) % nz, areas, nz)
        base0[k] = keep * (((6 - d) // 2) * per_interval + place * WORDS)
        base1[k] = keep * (((7 - d) // 2) * per_interval + place * WORDS)
        stride[k] = keep * per_interval
        odd[k] = d % 2
        return carry

    lax.fori_loop(0, slots, index_slot, 0)

    def clear(j, carry):
        words[pl.ds(j * 8, 8)] = jnp.zeros((8, 1, 128), jnp.int32)
        return carry

    lax.fori_loop(0, 2 * per_interval // 8, clear, 0)
    counts[...] = jnp.zeros_like(counts)

    sublane = lax.broadcasted_iota(jnp.int32, (8, 128), 0)
    lane = lax.broadcasted_iota(jnp.int32, (trials, 128), 1)
    bit = [jnp.left_shift(jnp.int32(1), sublane + 8 * j) for j in range(4)]
    unscale = [1.0 / b.astype(jnp.float32) for b in bit]

    own_row = static_row(area, 0, areas, nz)

    def groups(fired):
        return [fired[8 * q : 8 * q + 8] for q in range(trials // 8)]

    def fold(parts):
        total = functools.reduce(jnp.bitwise_or, parts)
        return jnp.sum(total, axis=0, keepdims=True)

    def store_words(gather, first, second):
        first, second = groups(first), groups(second)
        zero = jnp.zeros((8, 128), jnp.int32)

        def take(flags, bits):
            return [jnp.where(f, b, zero) for f, b in zip(flags, bits)]

        row = own_row
        landing[gather, row] = fold(take(first[:4], bit))
        landing[gather, row + 1] = fold(take(first[4:], bit[:2]) + take(second[4:], bit[2:]))
        landing[gather, row + 2] = fold(take(second[:4], bit))

    def send(gather, row, count, device, there, semaphore):
        return pltpu.make_async_remote_copy(
            src_ref=landing.at[gather, pl.ds(row, count * WORDS)],
            dst_ref=landing.at[gather, pl.ds(there, count * WORDS)],
            send_sem=send_sem.at[gather],
            recv_sem=semaphore,
            device_id=device,
            device_id_type=MESH,
        )

    def exchange(gather):
        far_first = sorted(range(1, nz), key=lambda dz: -ring_hops(dz, nz))
        for dz in far_first:
            there = static_row(area, z_place(nz - dz, nz), areas, nz)
            send(gather, own_row, 1, z_peer(dz), there, z_sem.at[gather, dz - 1]).start()

        for number, (first, count) in enumerate(batches(nz)):
            for place in range(first, first + count):
                offset = next(o for o in range(nz) if z_place(o, nz) == place)
                if offset:
                    row = static_row(area, place, areas, nz)
                    semaphore = z_sem.at[gather, nz - offset - 1]
                    send(gather, row, 1, z_peer(offset), row, semaphore).wait_recv()
            row = static_row(area, first, areas, nz)
            for offset in offsets:
                send(
                    gather, row, count, plane_peer(offset), row, plane_sem.at[gather, number]
                ).start()

        for number, (first, count) in enumerate(batches(nz)):
            arrived = (areas - 1) * count
            send(gather, 0, arrived, z_peer(1), 0, plane_sem.at[gather, number]).wait_recv()
            rows = areas * count * WORDS
            start = areas * first * WORDS
            step = min(8, areas) * count * WORDS

            def keep(j, carry):
                at = start + j * step
                words[pl.ds((gather + 2) * per_interval + at, step)] = landing[
                    gather, pl.ds(at, step)
                ]
                return carry

            lax.fori_loop(0, rows // step, keep, 0)

    leak = leak_ref[...]
    scale = jnp.ones(leak.shape, jnp.float32)
    for power in range(5):
        on = jnp.bitwise_and(leak, 1 << power) != 0
        scale = scale * jnp.where(on, jnp.float32(2.0 ** -(1 << power)), jnp.float32(1.0))
    drive = drive_ref[...].astype(jnp.float32)
    volt[...] = jnp.floor(membrane_ref[...])

    def initial(step):
        packed = bits_ref[trials * step : trials * (step + 1)]
        spread_out = jnp.broadcast_to(packed[:, 0:1], (trials, 128))
        for w in range(1, 4):
            spread_out = jnp.where(
                lane >= 32 * w, jnp.broadcast_to(packed[:, w : w + 1], (trials, 128)), spread_out
            )
        picked = jnp.bitwise_and(jnp.right_shift(spread_out, jnp.bitwise_and(lane, 31)), 1)
        return picked != 0

    store_words(0, initial(0), initial(1))
    pl.semaphore_wait(barrier, len(peers))

    def lhs_of(k, interval):
        s = odd[k]
        row0 = base0[k] + interval * stride[k]
        row1 = base1[k] + interval * stride[k]
        w0 = words[row0 + 2 * s]
        w1 = jnp.right_shift(words[row0 + 1], 16 * s)
        w2 = words[row1 + 2 * (1 - s)]
        w3 = jnp.right_shift(words[row1 + 1], 16 * (1 - s))
        parts = []
        for wide, narrow in ((w0, w1), (w2, w3)):
            wide = jnp.broadcast_to(wide, (8, 128))
            narrow = jnp.broadcast_to(narrow, (8, 128))
            parts += [jnp.bitwise_and(wide, b) for b in bit]
            parts += [jnp.bitwise_and(narrow, b) for b in bit[: trials // 8 - 4]]
        return jnp.concatenate(parts, axis=0).astype(jnp.float32).astype(jnp.bfloat16)

    def one_interval(interval, carry):
        exchange(interval)

        @pl.when(interval == 0)
        def _():
            load_weights.wait()

        total = jnp.zeros((2 * trials, 128), jnp.float32)
        for first in range(0, slots, SLOTS_PER_DOT):
            spikes = jnp.concatenate(
                [lhs_of(first + j, interval) for j in range(SLOTS_PER_DOT)], axis=1
            )
            synapses = weights[first : first + SLOTS_PER_DOT].reshape(SLOTS_PER_DOT * 128, 128)
            total = total + jnp.dot(spikes, synapses, preferred_element_type=jnp.float32)
        half = unscale + unscale[: trials // 8 - 4]
        total = total * jnp.concatenate(half + half, axis=0)

        voltage = volt[...]
        fired = []
        for step in range(DMIN):
            voltage = (
                voltage
                - jnp.floor(voltage * scale)
                + total[trials * step : trials * (step + 1)]
                + drive
            )
            flags = voltage >= THRESHOLD
            voltage = jnp.where(flags, 0.0, jnp.maximum(voltage, -THRESHOLD))
            fired.append(flags)
        volt[...] = voltage

        @pl.when(interval < intervals - 1)
        def _():
            store_words(interval + 1, *fired)

        for step in range(DMIN):
            row = jnp.sum(fired[step].astype(jnp.float32), axis=0, keepdims=True)
            counts[pl.ds(interval * DMIN + step, 1), :] = row
        return carry

    lax.fori_loop(0, intervals, one_interval, 0)
    out_membrane[...] = volt[...]

    rows16 = lax.broadcasted_iota(jnp.int32, (16, 128), 0)
    lanes16 = lax.broadcasted_iota(jnp.int32, (16, 128), 1)
    per_step = jnp.broadcast_to(jnp.sum(counts[...], axis=1, keepdims=True), (16, 128))
    own = jnp.sum(jnp.where(rows16 == lanes16, per_step, 0.0), axis=0, keepdims=True)
    own = jnp.where(
        lax.broadcasted_iota(jnp.int32, (nz, 128), 0) == rank, jnp.broadcast_to(own, (nz, 128)), 0.0
    )
    tile[...] = own
    sends = []
    for dz in range(1, nz):
        copy = pltpu.make_async_remote_copy(
            src_ref=tile,
            dst_ref=columns.at[dz - 1],
            send_sem=last_send_sem.at[dz - 1],
            recv_sem=last_z_sem.at[dz - 1],
            device_id=z_peer(dz),
            device_id_type=MESH,
        )
        copy.start()
        sends.append(copy)
    whole = own
    for dz in range(1, nz):
        sends[dz - 1].wait_recv()
        whole = whole + columns[dz - 1]
    totals[area] = whole
    for number, offset in enumerate(offsets):
        copy = pltpu.make_async_remote_copy(
            src_ref=totals.at[area],
            dst_ref=totals.at[area],
            send_sem=last_send_sem.at[nz - 1 + number],
            recv_sem=last_plane_sem,
            device_id=plane_peer(offset),
            device_id_type=MESH,
        )
        copy.start()
        sends.append(copy)
    pltpu.make_async_remote_copy(
        src_ref=totals.at[pl.ds(0, len(offsets))],
        dst_ref=totals.at[pl.ds(0, len(offsets))],
        send_sem=last_send_sem.at[0],
        recv_sem=last_plane_sem,
        device_id=z_peer(1),
        device_id_type=MESH,
    ).wait_recv()

    by_block = totals[...].reshape(blocks, 128)
    table = (
        area_ref[...] == lax.broadcasted_iota(jnp.int32, (blocks, 128), 1)
    ).astype(jnp.float32)
    sizes = jnp.sum(table, axis=0, keepdims=True) * float(trials * 128)
    by_area = lax.dot_general(
        by_block,
        table,
        (((0,), (0,)), ((), ())),
        precision=lax.Precision.HIGHEST,
        preferred_element_type=jnp.float32,
    )
    rates = by_area / sizes
    out_rates[...] = rates[:steps, :AREAS]

    for copy in sends:
        copy.wait_send()

    sent = nz - 1 + len(offsets) * nz

    def drain(gather, carry):
        send(gather, 0, sent, z_peer(1), 0, z_sem.at[gather, 0]).wait_send()
        return carry

    lax.fori_loop(0, intervals, drain, 0)


def on_device(
    dims, initial_bits, membrane, drive, leak_shift, weights, pre_block, block_mask, delay, area_of_block
):
    ny, nx, nc, nz, slots, trials, steps = dims
    blocks = ny * nx * nc * nz
    intervals = steps // DMIN
    smem = pl.BlockSpec(memory_space=pltpu.SMEM)
    vmem = pl.BlockSpec(memory_space=pltpu.VMEM)
    run = pl.pallas_call(
        functools.partial(kernel, dims),
        out_shape=(
            jax.ShapeDtypeStruct((trials, 128), jnp.float32),
            jax.ShapeDtypeStruct((steps, AREAS), jnp.float32),
        ),
        in_specs=[smem] * 3 + [vmem] * 5 + [pl.BlockSpec(memory_space=pl.ANY)],
        out_specs=(vmem, vmem),
        scratch_shapes=[
            pltpu.VMEM((slots, 128, 128), jnp.bfloat16),
            pltpu.VMEM((intervals, blocks * WORDS, 1, 128), jnp.int32),
            pltpu.VMEM(((intervals + 2) * blocks * WORDS, 1, 128), jnp.int32),
            pltpu.VMEM((trials, 128), jnp.float32),
            pltpu.VMEM((16, 128), jnp.float32),
            pltpu.VMEM((nz, 128), jnp.float32),
            pltpu.VMEM((nz - 1, nz, 128), jnp.float32),
            pltpu.VMEM((ny * nx * nc, nz, 128), jnp.float32),
            pltpu.SMEM((slots,), jnp.int32),
            pltpu.SMEM((slots,), jnp.int32),
            pltpu.SMEM((slots,), jnp.int32),
            pltpu.SMEM((slots,), jnp.int32),
            pltpu.SemaphoreType.DMA,
            pltpu.SemaphoreType.DMA((intervals,)),
            pltpu.SemaphoreType.DMA((intervals, nz - 1)),
            pltpu.SemaphoreType.DMA((intervals, len(batches(nz)))),
            pltpu.SemaphoreType.DMA((nz - 1 + ny * nx * nc - 1,)),
            pltpu.SemaphoreType.DMA((nz - 1,)),
            pltpu.SemaphoreType.DMA,
        ],
        compiler_params=pltpu.CompilerParams(
            collective_id=0, has_side_effects=True, vmem_limit_bytes=32 << 20
        ),
    )
    return run(
        pre_block.reshape(slots),
        block_mask.reshape(slots),
        delay.reshape(slots),
        initial_bits.reshape(DMIN * trials, 4),
        membrane,
        drive.reshape(1, 128),
        leak_shift.reshape(1, 128),
        area_of_block,
        weights.reshape(slots, 128, 128),
    )


def build(mesh, dims):
    both = ("area", "rank")
    return jax.shard_map(
        functools.partial(on_device, dims),
        mesh=mesh,
        in_specs=(
            P(None, None, both),
            P(None, both),
            P(both),
            P(both),
            P(both, None, None, None),
            P(both, None),
            P(both, None),
            P(both, None),
            P(),
        ),
        out_specs=(P(None, both), P()),
        check_vma=False,
    )


def solution(mesh):
    return build(mesh, (NY, NX, NC, mesh.shape["rank"], 128, 48, STEPS))
```

time: 478 us -> 89.2 us (0.19)
  the two profiles are of different devices: /device:TPU:32 before, /device:TPU:1 now
where the time goes in v1:
time: 89.2 us; the launch traced here: 88.9 us
  Pallas kernels  79.2 us (89%)
  local copies, waits for them, and re-layouts  8.99 us (10%)
    pallas_call x1, Pallas kernels, on_device(): run(pre_block.reshape(slots), block_mask.reshape(slots), delay.reshape(sl...  79.2 us
    unnamed x18, local copies, waits for them, and re-layouts  8.99 us

profile of v1, /device:TPU:1, one launch (start us, length us, event | category | flops | bytes accessed | tf_op | source)
XLA Modules:
  0.0 88.9 jit_solution(632525047895629864)
XLA Ops:
  0.6 0.8 copy.11
  1.4 0.8 copy.12.area_ref
  2.2 0.0 copy-start
  2.2 2.2 %copy-done = bf16[1,128,128,128]{3,2,1,0:T(8,128)(2,1)S(1)} copy-done((bf16[1,128,128,128]{3,2,1,0:T(8,128)(2,1)S(1)}, bf16[1,128,128,128]{3,2,1,0:T(8,128)(2,1)}, u32[]{:S(2)}) %copy-start) | copy-done | bytes 4194328
  4.4 0.0 copy-start.1
  4.4 0.7 copy-done.1
  5.2 0.0 copy-start.2
  5.2 0.7 copy-done.2
  5.8 0.0 copy-start.3
  5.8 0.7 copy-done.3
  6.5 0.0 copy-start.4
  6.5 0.7 copy-done.4
  7.1 0.0 copy-start.5
  7.1 0.7 copy-done.5
  7.8 0.0 copy-start.6
  7.8 0.7 copy-done.6
  8.4 79.2 %shard_map.104 = (f32[48,128]{1,0:T(8,128)S(1)}, f32[10,32]{1,0:T(8,128)S(1)}) custom-call(s32[128]{0:T(128)S(1)} %bitcast.9, s32[128]{0:T(128)S(1)} %bitcast.10, s32[128]{0:T(128)S(1)} %bitcast.11, s32[96,4]{1,0:T(8,128)S(1)} %bitcast.8, f32[48,128]{1,0:T(8,128)S(1)} %copy-done.1, s32[1,128]{1,0:T(1,128)S(1)} %bitcast.12, s32[1,128]{1,0:T(1,128)S(1)} %bitcast.13, ...), custom_call_target="tpu_custom_call" | custom-call | tf_op jit(solution)/shard_map/pallas_call | solution.py:401
  87.7 0.6 copy.15
  88.3 0.6 copy.16
Async XLA Ops:
  2.2 2.2 %copy-start = (bf16[1,128,128,128]{3,2,1,0:T(8,128)(2,1)S(1)}, bf16[1,128,128,128]{3,2,1,0:T(8,128)(2,1)}, u32[]{:S(2)}) copy-start(bf16[1,128,128,128]{3,2,1,0:T(8,128)(2,1)} %param.13) | copy-start | bytes 12582916
  4.4 0.7 copy-start.1
  5.2 0.7 copy-start.2
  5.8 0.7 copy-start.3
  6.5 0.7 copy-start.4
  7.1 0.7 copy-start.5
  7.8 0.7 copy-start.6

commit v2 on v1

--- a/solution.py
+++ b/solution.py
@@ -59,6 +59,17 @@
 
 def kernel(
     dims,
+    pre_hbm,
+    mask_hbm,
+    delay_hbm,
+    bits_hbm,
+    membrane_hbm,
+    drive_hbm,
+    leak_hbm,
+    area_hbm,
+    weights_hbm,
+    out_membrane,
+    out_rates,
     pre_ref,
     mask_ref,
     delay_ref,
@@ -67,9 +78,6 @@
     drive_ref,
     leak_ref,
     area_ref,
-    weights_hbm,
-    out_membrane,
-    out_rates,
     weights,
     landing,
     words,
@@ -78,10 +86,10 @@
     tile,
     columns,
     totals,
-    base0,
-    base1,
-    stride,
-    odd,
+    table_rows,
+    table,
+    input_sem,
+    table_sem,
     weights_sem,
     send_sem,
     z_sem,
@@ -113,19 +121,24 @@
     for peer in peers:
         pl.semaphore_signal(barrier, inc=1, device_id=peer, device_id_type=MESH)
 
+    inputs = [
+        (pre_hbm, pre_ref),
+        (mask_hbm, mask_ref),
+        (delay_hbm, delay_ref),
+        (bits_hbm, bits_ref),
+        (membrane_hbm, membrane_ref),
+        (drive_hbm, drive_ref),
+        (leak_hbm, leak_ref),
+        (area_hbm, area_ref),
+    ]
+    loads = [
+        pltpu.make_async_copy(source, target, input_sem.at[number])
+        for number, (source, target) in enumerate(inputs)
+    ]
+    for load in loads:
+        load.start()
     load_weights = pltpu.make_async_copy(weights_hbm, weights, weights_sem)
     load_weights.start()
-
-    def index_slot(k, carry):
-        d, keep, pre = delay_ref[k], mask_ref[k], pre_ref[k]
-        place = block_place(pre // nz, (pre % nz - rank + nz) % nz, areas, nz)
-        base0[k] = keep * (((6 - d) // 2) * per_interval + place * WORDS)
-        base1[k] = keep * (((7 - d) // 2) * per_interval + place * WORDS)
-        stride[k] = keep * per_interval
-        odd[k] = d % 2
-        return carry
-
-    lax.fori_loop(0, slots, index_slot, 0)
 
     def clear(j, carry):
         words[pl.ds(j * 8, 8)] = jnp.zeros((8, 1, 128), jnp.int32)
@@ -133,6 +146,17 @@
 
     lax.fori_loop(0, 2 * per_interval // 8, clear, 0)
     counts[...] = jnp.zeros_like(counts)
+    for load in loads:
+        load.wait()
+
+    pre, keep_slot, d = pre_ref[...], mask_ref[...], delay_ref[...]
+    place = block_place(pre // nz, (pre % nz - rank + nz) % nz, areas, nz)
+    table_rows[0:1] = keep_slot * (((6 - d) // 2) * per_interval + place * WORDS)
+    table_rows[1:2] = keep_slot * (((7 - d) // 2) * per_interval + place * WORDS)
+    table_rows[2:3] = keep_slot * per_interval
+    table_rows[3:4] = d % 2
+    load_table = pltpu.make_async_copy(table_rows, table, table_sem)
+    load_table.start()
 
     sublane = lax.broadcasted_iota(jnp.int32, (8, 128), 0)
     lane = lax.broadcasted_iota(jnp.int32, (trials, 128), 1)
@@ -214,7 +238,10 @@
     volt[...] = jnp.floor(membrane_ref[...])
 
     def initial(step):
-        packed = bits_ref[trials * step : trials * (step + 1)]
+        packed = bits_ref[step]
+        packed = jnp.concatenate([packed, jnp.zeros((4, trials), jnp.int32)], axis=0)
+        packed = jnp.concatenate([packed, jnp.zeros((8, 128 - trials), jnp.int32)], axis=1)
+        packed = jnp.transpose(packed)[:trials]
         spread_out = jnp.broadcast_to(packed[:, 0:1], (trials, 128))
         for w in range(1, 4):
             spread_out = jnp.where(
@@ -227,9 +254,9 @@
     pl.semaphore_wait(barrier, len(peers))
 
     def lhs_of(k, interval):
-        s = odd[k]
-        row0 = base0[k] + interval * stride[k]
-        row1 = base1[k] + interval * stride[k]
+        s = table[3, k]
+        row0 = table[0, k] + interval * table[2, k]
+        row1 = table[1, k] + interval * table[2, k]
         w0 = words[row0 + 2 * s]
         w1 = jnp.right_shift(words[row0 + 1], 16 * s)
         w2 = words[row1 + 2 * (1 - s)]
@@ -248,6 +275,7 @@
         @pl.when(interval == 0)
         def _():
             load_weights.wait()
+            load_table.wait()
 
         total = jnp.zeros((2 * trials, 128), jnp.float32)
         for first in range(0, slots, SLOTS_PER_DOT):
@@ -331,19 +359,27 @@
     ).wait_recv()
 
     by_block = totals[...].reshape(blocks, 128)
-    table = (
-        area_ref[...] == lax.broadcasted_iota(jnp.int32, (blocks, 128), 1)
+    area_row = jnp.broadcast_to(area_ref[...], (AREAS, blocks))
+    belongs = (
+        area_row == lax.broadcasted_iota(jnp.int32, (AREAS, blocks), 0)
     ).astype(jnp.float32)
-    sizes = jnp.sum(table, axis=0, keepdims=True) * float(trials * 128)
+    ones = jnp.ones((16, blocks), jnp.float32)
+    sizes = lax.dot_general(
+        ones,
+        belongs,
+        (((1,), (1,)), ((), ())),
+        precision=lax.Precision.HIGHEST,
+        preferred_element_type=jnp.float32,
+    ) * float(trials * 128)
     by_area = lax.dot_general(
-        by_block,
-        table,
-        (((0,), (0,)), ((), ())),
+        jnp.transpose(by_block)[:16],
+        belongs,
+        (((1,), (1,)), ((), ())),
         precision=lax.Precision.HIGHEST,
         preferred_element_type=jnp.float32,
     )
     rates = by_area / sizes
-    out_rates[...] = rates[:steps, :AREAS]
+    out_rates[...] = rates[:steps]
 
     for copy in sends:
         copy.wait_send()
@@ -363,7 +399,7 @@
     ny, nx, nc, nz, slots, trials, steps = dims
     blocks = ny * nx * nc * nz
     intervals = steps // DMIN
-    smem = pl.BlockSpec(memory_space=pltpu.SMEM)
+    hbm = pl.BlockSpec(memory_space=pl.ANY)
     vmem = pl.BlockSpec(memory_space=pltpu.VMEM)
     run = pl.pallas_call(
         functools.partial(kernel, dims),
@@ -371,9 +407,17 @@
             jax.ShapeDtypeStruct((trials, 128), jnp.float32),
             jax.ShapeDtypeStruct((steps, AREAS), jnp.float32),
         ),
-        in_specs=[smem] * 3 + [vmem] * 5 + [pl.BlockSpec(memory_space=pl.ANY)],
+        in_specs=[hbm] * 9,
         out_specs=(vmem, vmem),
         scratch_shapes=[
+            pltpu.VMEM((1, slots), jnp.int32),
+            pltpu.VMEM((1, slots), jnp.int32),
+            pltpu.VMEM((1, slots), jnp.int32),
+            pltpu.VMEM((DMIN, 4, trials), jnp.int32),
+            pltpu.VMEM((trials, 128), jnp.float32),
+            pltpu.VMEM((1, 128), jnp.int32),
+            pltpu.VMEM((1, 128), jnp.int32),
+            pltpu.VMEM((1, blocks), jnp.int32),
             pltpu.VMEM((slots, 128, 128), jnp.bfloat16),
             pltpu.VMEM((intervals, blocks * WORDS, 1, 128), jnp.int32),
             pltpu.VMEM(((intervals + 2) * blocks * WORDS, 1, 128), jnp.int32),
@@ -382,10 +426,10 @@
             pltpu.VMEM((nz, 128), jnp.float32),
             pltpu.VMEM((nz - 1, nz, 128), jnp.float32),
             pltpu.VMEM((ny * nx * nc, nz, 128), jnp.float32),
-            pltpu.SMEM((slots,), jnp.int32),
-            pltpu.SMEM((slots,), jnp.int32),
-            pltpu.SMEM((slots,), jnp.int32),
-            pltpu.SMEM((slots,), jnp.int32),
+            pltpu.VMEM((4, slots), jnp.int32),
+            pltpu.SMEM((4, slots), jnp.int32),
+            pltpu.SemaphoreType.DMA((8,)),
+            pltpu.SemaphoreType.DMA,
             pltpu.SemaphoreType.DMA,
             pltpu.SemaphoreType.DMA((intervals,)),
             pltpu.SemaphoreType.DMA((intervals, nz - 1)),
@@ -395,18 +439,18 @@
             pltpu.SemaphoreType.DMA,
         ],
         compiler_params=pltpu.CompilerParams(
-            collective_id=0, has_side_effects=True, vmem_limit_bytes=32 << 20
+            collective_id=0, has_side_effects=True, vmem_limit_bytes=60 << 20
         ),
     )
     return run(
-        pre_block.reshape(slots),
-        block_mask.reshape(slots),
-        delay.reshape(slots),
-        initial_bits.reshape(DMIN * trials, 4),
+        pre_block,
+        block_mask,
+        delay,
+        jnp.transpose(initial_bits, (0, 2, 1)),
         membrane,
         drive.reshape(1, 128),
         leak_shift.reshape(1, 128),
-        area_of_block,
+        area_of_block.reshape(1, blocks),
         weights.reshape(slots, 128, 128),
     )
 

time: 89.2 us -> 79.6 us (0.89)
  local copies, waits for them, and re-layouts: 8.99 us -> 2.64 us
  Pallas kernels: 79.2 us -> 76.2 us
    unnamed x18 -> x2, local copies, waits for them, and re-layouts: 8.99 us -> 2.64 us
    pallas_call x1, Pallas kernels: 79.2 us -> 76.2 us  [on_device(): run(pre_block, block_mask, delay, jnp.transpose(initial_bits, (0, 2, 1)),...]
where the time goes in v2:
time: 79.6 us; the launch traced here: 79.4 us
  Pallas kernels  76.2 us (96%)
  local copies, waits for them, and re-layouts  2.64 us (3%)
    pallas_call x1, Pallas kernels, on_device(): run(pre_block, block_mask, delay, jnp.transpose(initial_bits, (0, 2, 1)),...  76.2 us
    unnamed x2, local copies, waits for them, and re-layouts  2.64 us

profile of v2, /device:TPU:1, one launch (start us, length us, event | category | flops | bytes accessed | tf_op | source)
XLA Modules:
  0.0 79.4 jit_solution(12526788154502525359)
XLA Ops:
  0.6 76.2 %shard_map.104 = (f32[48,128]{1,0:T(8,128)}, f32[10,32]{1,0:T(8,128)}) custom-call(s32[1,128]{1,0:T(1,128)} %pre_hbm.1, s32[1,128]{1,0:T(1,128)} %mask_hbm.1, s32[1,128]{1,0:T(1,128)} %delay_hbm.1, s32[2,4,48]{2,1,0:T(4,128)} %bitcast.6, f32[48,128]{1,0:T(8,128)} %membrane_hbm.1, s32[1,128]{1,0:T(1,128)} %bitcast.8, s32[1,128]{1,0:T(1,128)} %bitcast.9, ...), custom_call_target="tpu_custom_call" | custom-call | tf_op jit(solution)/shard_map/pallas_call | solution.py:445
  76.8 1.3 %copy.13 = f32[48,128]{1,0:T(8,128)} copy(f32[48,128]{1,0:T(8,128)} %get-tuple-element.4) | data formatting | bytes 49152
  78.1 1.3 %copy.14 = f32[10,32]{1,0:T(8,128)} copy(f32[10,32]{1,0:T(8,128)} %get-tuple-element.5) | data formatting | bytes 2560

commit v3 on v2

--- a/solution.py
+++ b/solution.py
@@ -83,9 +83,6 @@
     words,
     volt,
     counts,
-    tile,
-    columns,
-    totals,
     table_rows,
     table,
     input_sem,
@@ -94,9 +91,6 @@
     send_sem,
     z_sem,
     plane_sem,
-    last_send_sem,
-    last_z_sem,
-    last_plane_sem,
 ):
     ny, nx, nc, nz, slots, trials, steps = dims
     areas = ny * nx * nc
@@ -251,7 +245,25 @@
         return picked != 0
 
     store_words(0, initial(0), initial(1))
+    lane_area = lax.broadcasted_iota(jnp.int32, (128, blocks), 0) % AREAS
+    belongs = (jnp.broadcast_to(area_ref[...], (128, blocks)) == lane_area).astype(jnp.float32)
+    sizes = lax.dot_general(
+        jnp.ones((8, blocks), jnp.float32),
+        belongs,
+        (((1,), (1,)), ((), ())),
+        precision=lax.Precision.HIGHEST,
+        preferred_element_type=jnp.float32,
+    )[0:1] * float(trials * 128)
+    block_lane = lax.broadcasted_iota(jnp.int32, (1, blocks), 1)
+    own_area = jnp.sum(
+        jnp.where(block_lane == area * nz + rank, area_ref[...], 0), axis=1, keepdims=True
+    )
+    lanes = lax.broadcasted_iota(jnp.int32, (1, 128), 1)
+    own_lanes = lanes % AREAS == own_area
     pl.semaphore_wait(barrier, len(peers))
+    exchange(0)
+    load_weights.wait()
+    load_table.wait()
 
     def lhs_of(k, interval):
         s = table[3, k]
@@ -270,13 +282,6 @@
         return jnp.concatenate(parts, axis=0).astype(jnp.float32).astype(jnp.bfloat16)
 
     def one_interval(interval, carry):
-        exchange(interval)
-
-        @pl.when(interval == 0)
-        def _():
-            load_weights.wait()
-            load_table.wait()
-
         total = jnp.zeros((2 * trials, 128), jnp.float32)
         for first in range(0, slots, SLOTS_PER_DOT):
             spikes = jnp.concatenate(
@@ -301,96 +306,59 @@
             fired.append(flags)
         volt[...] = voltage
 
+        for step in range(DMIN):
+            row = jnp.sum(fired[step].astype(jnp.float32), axis=0, keepdims=True)
+            counts[pl.ds(interval * DMIN + step, 1), :] = row
+
         @pl.when(interval < intervals - 1)
         def _():
             store_words(interval + 1, *fired)
 
-        for step in range(DMIN):
-            row = jnp.sum(fired[step].astype(jnp.float32), axis=0, keepdims=True)
-            counts[pl.ds(interval * DMIN + step, 1), :] = row
+        @pl.when(interval == intervals - 1)
+        def _():
+            per_step = jnp.sum(counts[...], axis=1, keepdims=True).astype(jnp.int32)
+            for r in range(WORDS):
+                row = jnp.zeros((1, 128), jnp.int32)
+                for j in range(4):
+                    here = own_lanes & (lanes // AREAS == j)
+                    row = jnp.where(here, per_step[4 * r + j : 4 * r + j + 1], row)
+                landing[intervals, own_row + r] = row
+
+        exchange(interval + 1)
         return carry
 
     lax.fori_loop(0, intervals, one_interval, 0)
     out_membrane[...] = volt[...]
 
-    rows16 = lax.broadcasted_iota(jnp.int32, (16, 128), 0)
-    lanes16 = lax.broadcasted_iota(jnp.int32, (16, 128), 1)
-    per_step = jnp.broadcast_to(jnp.sum(counts[...], axis=1, keepdims=True), (16, 128))
-    own = jnp.sum(jnp.where(rows16 == lanes16, per_step, 0.0), axis=0, keepdims=True)
-    own = jnp.where(
-        lax.broadcasted_iota(jnp.int32, (nz, 128), 0) == rank, jnp.broadcast_to(own, (nz, 128)), 0.0
-    )
-    tile[...] = own
-    sends = []
-    for dz in range(1, nz):
-        copy = pltpu.make_async_remote_copy(
-            src_ref=tile,
-            dst_ref=columns.at[dz - 1],
-            send_sem=last_send_sem.at[dz - 1],
-            recv_sem=last_z_sem.at[dz - 1],
-            device_id=z_peer(dz),
-            device_id_type=MESH,
-        )
-        copy.start()
-        sends.append(copy)
-    whole = own
-    for dz in range(1, nz):
-        sends[dz - 1].wait_recv()
-        whole = whole + columns[dz - 1]
-    totals[area] = whole
-    for number, offset in enumerate(offsets):
-        copy = pltpu.make_async_remote_copy(
-            src_ref=totals.at[area],
-            dst_ref=totals.at[area],
-            send_sem=last_send_sem.at[nz - 1 + number],
-            recv_sem=last_plane_sem,
-            device_id=plane_peer(offset),
-            device_id_type=MESH,
-        )
-        copy.start()
-        sends.append(copy)
-    pltpu.make_async_remote_copy(
-        src_ref=totals.at[pl.ds(0, len(offsets))],
-        dst_ref=totals.at[pl.ds(0, len(offsets))],
-        send_sem=last_send_sem.at[0],
-        recv_sem=last_plane_sem,
-        device_id=z_peer(1),
-        device_id_type=MESH,
-    ).wait_recv()
-
-    by_block = totals[...].reshape(blocks, 128)
-    area_row = jnp.broadcast_to(area_ref[...], (AREAS, blocks))
-    belongs = (
-        area_row == lax.broadcasted_iota(jnp.int32, (AREAS, blocks), 0)
-    ).astype(jnp.float32)
-    ones = jnp.ones((16, blocks), jnp.float32)
-    sizes = lax.dot_general(
-        ones,
-        belongs,
-        (((1,), (1,)), ((), ())),
-        precision=lax.Precision.HIGHEST,
-        preferred_element_type=jnp.float32,
-    ) * float(trials * 128)
-    by_area = lax.dot_general(
-        jnp.transpose(by_block)[:16],
-        belongs,
-        (((1,), (1,)), ((), ())),
-        precision=lax.Precision.HIGHEST,
-        preferred_element_type=jnp.float32,
-    )
-    rates = by_area / sizes
-    out_rates[...] = rates[:steps]
-
-    for copy in sends:
-        copy.wait_send()
-
+    def add_counts(j, total):
+        at = (intervals + 2) * per_interval + j * 8 * WORDS
+        return total + words[pl.ds(at, 8 * WORDS)]
+
+    summed = lax.fori_loop(
+        0, blocks // 8, add_counts, jnp.zeros((8 * WORDS, 1, 128), jnp.int32)
+    ).reshape(8, WORDS, 128)
+    rates = jnp.sum(summed, axis=0).astype(jnp.float32) / sizes
+    for step in range(steps):
+        lane0 = AREAS * (step % 4)
+        out_rates[step : step + 1] = rates[step // 4 : step // 4 + 1, lane0 : lane0 + AREAS]
     sent = nz - 1 + len(offsets) * nz
 
     def drain(gather, carry):
         send(gather, 0, sent, z_peer(1), 0, z_sem.at[gather, 0]).wait_send()
         return carry
 
-    lax.fori_loop(0, intervals, drain, 0)
+    lax.fori_loop(0, intervals + 1, drain, 0)
+
+
+def write_out(membrane, rates, out_membrane, out_rates, sem):
+    copies = [
+        pltpu.make_async_copy(membrane, out_membrane, sem.at[0]),
+        pltpu.make_async_copy(rates, out_rates, sem.at[1]),
+    ]
+    for copy in copies:
+        copy.start()
+    for copy in copies:
+        copy.wait()
 
 
 def on_device(
@@ -399,14 +367,15 @@
     ny, nx, nc, nz, slots, trials, steps = dims
     blocks = ny * nx * nc * nz
     intervals = steps // DMIN
-    hbm = pl.BlockSpec(memory_space=pl.ANY)
+    hbm = pl.BlockSpec(memory_space=pltpu.HBM)
     vmem = pl.BlockSpec(memory_space=pltpu.VMEM)
+    shapes = (
+        jax.ShapeDtypeStruct((trials, 128), jnp.float32),
+        jax.ShapeDtypeStruct((steps, AREAS), jnp.float32),
+    )
     run = pl.pallas_call(
         functools.partial(kernel, dims),
-        out_shape=(
-            jax.ShapeDtypeStruct((trials, 128), jnp.float32),
-            jax.ShapeDtypeStruct((steps, AREAS), jnp.float32),
-        ),
+        out_shape=shapes,
         in_specs=[hbm] * 9,
         out_specs=(vmem, vmem),
         scratch_shapes=[
@@ -419,30 +388,24 @@
             pltpu.VMEM((1, 128), jnp.int32),
             pltpu.VMEM((1, blocks), jnp.int32),
             pltpu.VMEM((slots, 128, 128), jnp.bfloat16),
-            pltpu.VMEM((intervals, blocks * WORDS, 1, 128), jnp.int32),
-            pltpu.VMEM(((intervals + 2) * blocks * WORDS, 1, 128), jnp.int32),
+            pltpu.VMEM((intervals + 1, blocks * WORDS, 1, 128), jnp.int32),
+            pltpu.VMEM(((intervals + 3) * blocks * WORDS, 1, 128), jnp.int32),
             pltpu.VMEM((trials, 128), jnp.float32),
             pltpu.VMEM((16, 128), jnp.float32),
-            pltpu.VMEM((nz, 128), jnp.float32),
-            pltpu.VMEM((nz - 1, nz, 128), jnp.float32),
-            pltpu.VMEM((ny * nx * nc, nz, 128), jnp.float32),
             pltpu.VMEM((4, slots), jnp.int32),
             pltpu.SMEM((4, slots), jnp.int32),
             pltpu.SemaphoreType.DMA((8,)),
             pltpu.SemaphoreType.DMA,
             pltpu.SemaphoreType.DMA,
-            pltpu.SemaphoreType.DMA((intervals,)),
-            pltpu.SemaphoreType.DMA((intervals, nz - 1)),
-            pltpu.SemaphoreType.DMA((intervals, len(batches(nz)))),
-            pltpu.SemaphoreType.DMA((nz - 1 + ny * nx * nc - 1,)),
-            pltpu.SemaphoreType.DMA((nz - 1,)),
-            pltpu.SemaphoreType.DMA,
+            pltpu.SemaphoreType.DMA((intervals + 1,)),
+            pltpu.SemaphoreType.DMA((intervals + 1, nz - 1)),
+            pltpu.SemaphoreType.DMA((intervals + 1, len(batches(nz)))),
         ],
         compiler_params=pltpu.CompilerParams(
-            collective_id=0, has_side_effects=True, vmem_limit_bytes=60 << 20
+            collective_id=0, has_side_effects=True, vmem_limit_bytes=40 << 20
         ),
     )
-    return run(
+    operands = (
         pre_block,
         block_mask,
         delay,
@@ -453,6 +416,15 @@
         area_of_block.reshape(1, blocks),
         weights.reshape(slots, 128, 128),
     )
+    result = run(*[pltpu.with_memory_space_constraint(x, pltpu.HBM) for x in operands])
+    return pl.pallas_call(
+        write_out,
+        out_shape=shapes,
+        in_specs=[vmem, vmem],
+        out_specs=(hbm, hbm),
+        scratch_shapes=[pltpu.SemaphoreType.DMA((2,))],
+        compiler_params=pltpu.CompilerParams(vmem_limit_bytes=1 << 20),
+    )(*result)
 
 
 def build(mesh, dims):

time: 79.6 us -> 77.2 us (0.970)
  local copies, waits for them, and re-layouts: 2.64 us -> 0 us
    unnamed x2 -> x0, local copies, waits for them, and re-layouts: 2.64 us -> none
    pallas_call x1 -> x2, Pallas kernels: 76.2 us -> 76.5 us  [the longest x1 75.9 us: on_device(): run(*[pltpu.with_memory_space_constraint(x, pltpu.HBM) for x in operands])]
where the time goes in v3:
time: 77.2 us; the launch traced here: 77.1 us
  Pallas kernels  76.5 us (99%)
    pallas_call x1, Pallas kernels, on_device(): run(*[pltpu.with_memory_space_constraint(x, pltpu.HBM) for x in operands])  75.9 us

profile of v3, /device:TPU:1, one launch (start us, length us, event | category | flops | bytes accessed | tf_op | source)
XLA Modules:
  0.0 77.1 jit_solution(6527233422113987956)
XLA Ops:
  0.6 75.9 %shard_map.104 = (f32[48,128]{1,0:T(8,128)S(1)}, f32[10,32]{1,0:T(8,128)S(1)}) custom-call(s32[1,128]{1,0:T(1,128)} %pre_hbm.1, s32[1,128]{1,0:T(1,128)} %mask_hbm.1, s32[1,128]{1,0:T(1,128)} %delay_hbm.1, s32[2,4,48]{2,1,0:T(4,128)} %bitcast.6, f32[48,128]{1,0:T(8,128)} %membrane_hbm.1, s32[1,128]{1,0:T(1,128)} %bitcast.8, s32[1,128]{1,0:T(1,128)} %bitcast.9, ...), custom_call_target="tpu_custom_call" | custom-call | tf_op jit(solution)/shard_map/pallas_call | solution.py:419
  76.5 0.6 shard_map.105

commit v4 on v3

--- a/solution.py
+++ b/solution.py
@@ -18,8 +18,8 @@
 
 
 def batches(nz):
-    pairs = [(2 * near - 1, 2) for near in range(1, nz // 2 - 1)]
-    return [(0, 1)] + pairs + [(nz - 3, 3)]
+    pairs = [(2 * near - 1, 2) for near in range(1, nz // 2)]
+    return [(0, 1)] + pairs + [(nz - 1, 1)]
 
 
 def z_place(offset, nz):
@@ -28,12 +28,9 @@
 
 def block_place(area, offset, areas, nz):
     place = jnp.where(offset > nz // 2, 2 * (nz - offset), jnp.maximum(2 * offset - 1, 0))
-    first = jnp.where(place % 2 == 1, place, place - 1)
-    count = jnp.where(place == 0, 1, 2)
-    first = jnp.where(place == 0, 0, first)
-    last = place >= nz - 3
-    first = jnp.where(last, nz - 3, first)
-    count = jnp.where(last, 3, count)
+    single = (place == 0) | (place == nz - 1)
+    first = jnp.where(single | (place % 2 == 1), place, place - 1)
+    count = jnp.where(single, 1, 2)
     return first * areas + area * count + place - first
 
 
@@ -188,24 +185,47 @@
             device_id_type=MESH,
         )
 
-    def exchange(gather):
+    def offset_at(place):
+        return next(o for o in range(nz) if z_place(o, nz) == place)
+
+    def plane_hops(offset):
+        return ring_hops(offset[0], ny) + ring_hops(offset[1], nx)
+
+    def goes_direct(dz, offset):
+        hops = ring_hops(dz, nz)
+        return hops == 1 or hops + plane_hops(offset) >= ny // 2 + nx // 2 + nz // 2 - 1
+
+    def exchange(gather, with_direct):
         far_first = sorted(range(1, nz), key=lambda dz: -ring_hops(dz, nz))
         for dz in far_first:
             there = static_row(area, z_place(nz - dz, nz), areas, nz)
             send(gather, own_row, 1, z_peer(dz), there, z_sem.at[gather, dz - 1]).start()
 
+        direct = [
+            (dz, o) for dz in range(1, nz) for o in offsets if with_direct and goes_direct(dz, o)
+        ]
+        for dz, offset in sorted(direct, key=lambda p: -(ring_hops(p[0], nz) + plane_hops(p[1]))):
+            place = z_place(nz - dz, nz)
+            number = next(n for n, (f, c) in enumerate(batches(nz)) if f <= place < f + c)
+            device = (plane_peer(offset)[0], z_peer(dz)[1])
+            there = static_row(area, place, areas, nz)
+            send(gather, own_row, 1, device, there, plane_sem.at[gather, number]).start()
+
         for number, (first, count) in enumerate(batches(nz)):
-            for place in range(first, first + count):
-                offset = next(o for o in range(nz) if z_place(o, nz) == place)
+            places = range(first, first + count)
+            for place in places:
+                offset = offset_at(place)
                 if offset:
                     row = static_row(area, place, areas, nz)
                     semaphore = z_sem.at[gather, nz - offset - 1]
                     send(gather, row, 1, z_peer(offset), row, semaphore).wait_recv()
             row = static_row(area, first, areas, nz)
             for offset in offsets:
-                send(
-                    gather, row, count, plane_peer(offset), row, plane_sem.at[gather, number]
-                ).start()
+                dz = offset_at(first)
+                if not (with_direct and dz and goes_direct(dz, offset)):
+                    send(
+                        gather, row, count, plane_peer(offset), row, plane_sem.at[gather, number]
+                    ).start()
 
         for number, (first, count) in enumerate(batches(nz)):
             arrived = (areas - 1) * count
@@ -261,7 +281,7 @@
     lanes = lax.broadcasted_iota(jnp.int32, (1, 128), 1)
     own_lanes = lanes % AREAS == own_area
     pl.semaphore_wait(barrier, len(peers))
-    exchange(0)
+    exchange(0, False)
     load_weights.wait()
     load_table.wait()
 
@@ -324,7 +344,7 @@
                     row = jnp.where(here, per_step[4 * r + j : 4 * r + j + 1], row)
                 landing[intervals, own_row + r] = row
 
-        exchange(interval + 1)
+        exchange(interval + 1, True)
         return carry
 
     lax.fori_loop(0, intervals, one_interval, 0)

time: 77.2 us -> 73.6 us (0.953)
  Pallas kernels: 76.5 us -> 72.9 us
    pallas_call x1, Pallas kernels: 75.9 us -> 72.2 us  [on_device(): run(*[pltpu.with_memory_space_constraint(x, pltpu.HBM) for x in operands])]
where the time goes in v4:
time: 73.6 us; the launch traced here: 73.5 us
  Pallas kernels  72.9 us (99%)
    pallas_call x1, Pallas kernels, on_device(): run(*[pltpu.with_memory_space_constraint(x, pltpu.HBM) for x in operands])  72.2 us

profile of v4, /device:TPU:1, one launch (start us, length us, event | category | flops | bytes accessed | tf_op | source)
XLA Modules:
  0.0 73.5 jit_solution(5549894652110235339)
XLA Ops:
  0.6 72.2 %shard_map.104 = (f32[48,128]{1,0:T(8,128)S(1)}, f32[10,32]{1,0:T(8,128)S(1)}) custom-call(s32[1,128]{1,0:T(1,128)} %pre_hbm.1, s32[1,128]{1,0:T(1,128)} %mask_hbm.1, s32[1,128]{1,0:T(1,128)} %delay_hbm.1, s32[2,4,48]{2,1,0:T(4,128)} %bitcast.6, f32[48,128]{1,0:T(8,128)} %membrane_hbm.1, s32[1,128]{1,0:T(1,128)} %bitcast.8, s32[1,128]{1,0:T(1,128)} %bitcast.9, ...), custom_call_target="tpu_custom_call" | custom-call | tf_op jit(solution)/shard_map/pallas_call | solution.py:439
  72.9 0.6 shard_map.105

commit v5 on v4

--- a/solution.py
+++ b/solution.py
@@ -26,7 +26,12 @@
     return 2 * (nz - offset) if offset > nz // 2 else max(2 * offset - 1, 0)
 
 
+def core_major(area, areas):
+    return (area % NC) * (areas // NC) + area // NC
+
+
 def block_place(area, offset, areas, nz):
+    area = core_major(area, areas)
     place = jnp.where(offset > nz // 2, 2 * (nz - offset), jnp.maximum(2 * offset - 1, 0))
     single = (place == 0) | (place == nz - 1)
     first = jnp.where(single | (place % 2 == 1), place, place - 1)
@@ -35,6 +40,7 @@
 
 
 def static_row(area, place, areas, nz):
+    area = core_major(area, areas)
     first, count = next(b for b in batches(nz) if b[0] <= place < b[0] + b[1])
     return (first * areas + area * count + place - first) * WORDS
 
@@ -88,6 +94,7 @@
     send_sem,
     z_sem,
     plane_sem,
+    twin_sem,
 ):
     ny, nx, nc, nz, slots, trials, steps = dims
     areas = ny * nx * nc
@@ -191,9 +198,15 @@
     def plane_hops(offset):
         return ring_hops(offset[0], ny) + ring_hops(offset[1], nx)
 
+    def by_twin(dz):
+        return ring_hops(dz, nz) <= nz // 4
+
     def goes_direct(dz, offset):
-        hops = ring_hops(dz, nz)
-        return hops == 1 or hops + plane_hops(offset) >= ny // 2 + nx // 2 + nz // 2 - 1
+        far = ring_hops(dz, nz) + plane_hops(offset) >= ny // 2 + nx // 2 + nz // 2 - 1
+        return by_twin(dz) or far
+
+    def plane_of(dz):
+        return [o for o in offsets if o[2] == 0] if by_twin(dz) else offsets
 
     def exchange(gather, with_direct):
         far_first = sorted(range(1, nz), key=lambda dz: -ring_hops(dz, nz))
@@ -202,7 +215,10 @@
             send(gather, own_row, 1, z_peer(dz), there, z_sem.at[gather, dz - 1]).start()
 
         direct = [
-            (dz, o) for dz in range(1, nz) for o in offsets if with_direct and goes_direct(dz, o)
+            (dz, o)
+            for dz in range(1, nz)
+            for o in plane_of(dz)
+            if with_direct and goes_direct(dz, o)
         ]
         for dz, offset in sorted(direct, key=lambda p: -(ring_hops(p[0], nz) + plane_hops(p[1]))):
             place = z_place(nz - dz, nz)
@@ -220,16 +236,31 @@
                     semaphore = z_sem.at[gather, nz - offset - 1]
                     send(gather, row, 1, z_peer(offset), row, semaphore).wait_recv()
             row = static_row(area, first, areas, nz)
-            for offset in offsets:
-                dz = offset_at(first)
+            dz = offset_at(first)
+            for offset in plane_of(dz):
                 if not (with_direct and dz and goes_direct(dz, offset)):
                     send(
                         gather, row, count, plane_peer(offset), row, plane_sem.at[gather, number]
                     ).start()
 
+        half = areas // nc
+
+        def wait_plane(number, blocks_in):
+            send(gather, 0, blocks_in, z_peer(1), 0, plane_sem.at[gather, number]).wait_recv()
+
         for number, (first, count) in enumerate(batches(nz)):
-            arrived = (areas - 1) * count
-            send(gather, 0, arrived, z_peer(1), 0, plane_sem.at[gather, number]).wait_recv()
+            if by_twin(offset_at(first)):
+                wait_plane(number, (half - 1) * count)
+                row = (first * areas + core * half * count) * WORDS
+                semaphore = twin_sem.at[gather, number]
+                send(gather, row, half * count, plane_peer((0, 0, 1)), row, semaphore).start()
+
+        for number, (first, count) in enumerate(batches(nz)):
+            if by_twin(offset_at(first)):
+                semaphore = twin_sem.at[gather, number]
+                send(gather, 0, half * count, z_peer(1), 0, semaphore).wait_recv()
+            else:
+                wait_plane(number, (areas - 1) * count)
             rows = areas * count * WORDS
             start = areas * first * WORDS
             step = min(8, areas) * count * WORDS
@@ -361,7 +392,7 @@
     for step in range(steps):
         lane0 = AREAS * (step % 4)
         out_rates[step : step + 1] = rates[step // 4 : step // 4 + 1, lane0 : lane0 + AREAS]
-    sent = nz - 1 + len(offsets) * nz
+    sent = blocks - 1
 
     def drain(gather, carry):
         send(gather, 0, sent, z_peer(1), 0, z_sem.at[gather, 0]).wait_send()
@@ -420,6 +451,7 @@
             pltpu.SemaphoreType.DMA((intervals + 1,)),
             pltpu.SemaphoreType.DMA((intervals + 1, nz - 1)),
             pltpu.SemaphoreType.DMA((intervals + 1, len(batches(nz)))),
+            pltpu.SemaphoreType.DMA((intervals + 1, len(batches(nz)))),
         ],
         compiler_params=pltpu.CompilerParams(
             collective_id=0, has_side_effects=True, vmem_limit_bytes=40 << 20

time: 73.6 us -> 73.3 us (level)
  no operation moved by 1% of the time
where the time goes in v5:
time: 73.3 us; the launch traced here: 73.2 us
  Pallas kernels  72.5 us (99%)
    pallas_call x1, Pallas kernels, on_device(): run(*[pltpu.with_memory_space_constraint(x, pltpu.HBM) for x in operands])  71.9 us

profile of v5, /device:TPU:1, one launch (start us, length us, event | category | flops | bytes accessed | tf_op | source)
XLA Modules:
  0.0 73.2 jit_solution(15015011445253195452)
XLA Ops:
  0.6 71.9 %shard_map.104 = (f32[48,128]{1,0:T(8,128)S(1)}, f32[10,32]{1,0:T(8,128)S(1)}) custom-call(s32[1,128]{1,0:T(1,128)} %pre_hbm.1, s32[1,128]{1,0:T(1,128)} %mask_hbm.1, s32[1,128]{1,0:T(1,128)} %delay_hbm.1, s32[2,4,48]{2,1,0:T(4,128)} %bitcast.6, f32[48,128]{1,0:T(8,128)} %membrane_hbm.1, s32[1,128]{1,0:T(1,128)} %bitcast.8, s32[1,128]{1,0:T(1,128)} %bitcast.9, ...), custom_call_target="tpu_custom_call" | custom-call | tf_op jit(solution)/shard_map/pallas_call | solution.py:471
  72.5 0.6 shard_map.105
